TPU v7x, 32 devices: a whole 2x2x4 slice. The times are simulated.
32 devices in a mesh: north: 8 (over y, x, core), deep: 4 (over z).
Axes of the slice: x: 2, y: 2, z: 4, core: 2. Of those that a mesh axis runs over, the one named last changes fastest.
Arguments:
- velocity: float32 [4, 128, 64, 256], P(None, None, 'north', 'deep'), may hold values from -6 to 6
- coupling: float32 [4, 4], replicated, may hold values from -4 to 4
- symbol_x: float32 [128], replicated, may hold values from 0.3 to 3
- symbol_y: float32 [64], replicated, may hold values from 0.3 to 3
- symbol_z: float32 [256], replicated, may hold values from 0.3 to 3
Outputs:
- spectrum: float32 [4, 128, 64, 256], P(None, 'north', 'deep')
All inputs are finite; a program needn't handle non-finite values.
Results may differ from a plain program's by a relative error of at most 0.00007.
Values sent between devices are 32-bit elements; how exact they have to be, the bound alone decides.
A program may use at most 128 MiB of HBM per device.

v0:
```python
import functools

import jax
import jax.numpy as jnp
import numpy as np
from jax import lax
from jax.experimental import pallas as pl
from jax.experimental.pallas import tpu as pltpu
from jax.sharding import PartitionSpec as P

LANES = 128
SIZES = (1, 1, 2, 4, 2, 2, 2, 2)
EARLY = 2
HOLD = 4
F32 = jnp.float32
BF16 = jnp.bfloat16
MESH = pl.DeviceIdType.MESH


def basis_table(count):
    rank = np.arange(1, count + 1)
    turns = (rank[:, None] * rank[None, :]) % (2 * count + 2)
    table = np.sin(np.pi / (count + 1) * turns) * (2.0 / (count + 1)) ** 0.5
    table = table.astype(np.float32)
    high = table.astype(jnp.bfloat16)
    low = (table - high.astype(np.float32)).astype(jnp.bfloat16)
    return high, low


def split(values):
    high = values.astype(BF16)
    low = (values - high.astype(F32)).astype(BF16)
    return high, low


def plan(chunks, packs):
    starts = [sum(chunks[:c]) for c in range(len(chunks))]
    early = min(EARLY, len(chunks))
    pieces = [(p, 1, starts[c], chunks[c]) for p in range(packs) for c in range(early)]
    pieces += [(0, packs, starts[c], chunks[c]) for c in range(early, len(chunks))]
    owner = list(range(early)) * packs + list(range(early, len(chunks)))
    return starts, early, pieces, owner


def kernel(
    north, deep, chunks,
    a_hbm, coupling_hbm, sym_x_hbm, sym_y_hbm, sym_z_hbm, tx_hbm, ty_hbm, tz_hbm,
    out,
    a, coupling, sym_x, sym_y, sym_z, tx, ty, tz, x1, r, s, t,
    load_sem, send_n, recv_n, send_d, recv_d, ready,
):
    me_n = lax.axis_index("north")
    me_d = lax.axis_index("deep")
    fields, share_y, share_z, size_x = a.shape
    pack = LANES // share_z
    packs = fields // pack
    share_x = size_x // north
    size_y = share_y * north
    block_y = size_y // deep
    size_z = share_z * deep
    starts, early, pieces, owner = plan(chunks, packs)
    half = deep // 2
    odd = lax.rem(me_n, 2)

    loads = [pltpu.make_async_copy(tx_hbm, tx, load_sem.at[0])]
    for p in range(packs):
        part = pl.ds(p * pack, pack)
        loads.append(pltpu.make_async_copy(a_hbm.at[part], a.at[part], load_sem.at[1 + p]))
    pairs = [
        (ty_hbm, ty), (sym_x_hbm, sym_x), (sym_y_hbm, sym_y), (sym_z_hbm, sym_z),
        (coupling_hbm, coupling), (tz_hbm, tz),
    ]
    late = [
        pltpu.make_async_copy(source, target, load_sem.at[len(loads) + i])
        for i, (source, target) in enumerate(pairs)
    ]
    for copy in loads + late:
        copy.start()

    peers_n = [lax.rem(me_n + k, north) for k in range(1, north)]
    side = me_d // half
    across = [(1 - side) * half + j for j in range(half)]
    along = [side * half + lax.rem(me_d + j, half) for j in range(1, half)]
    peers_d = across + along

    barrier = pltpu.get_barrier_semaphore()
    for k in range(0, north, 2):
        even = lax.rem(me_n - odd + k, north)

        @pl.when(even != me_n)
        def _():
            pl.semaphore_signal(barrier, inc=1, device_id={"north": even}, device_id_type=MESH)

    for peer in peers_d:
        pl.semaphore_signal(
            barrier, inc=1, device_id={"north": me_n - odd + 1, "deep": peer}, device_id_type=MESH
        )

    def enter_north():
        @pl.when(odd == 0)
        def _():
            pl.semaphore_wait(barrier, north - 1)
            pl.semaphore_signal(ready, inc=1, device_id={"north": me_n + 1}, device_id_type=MESH)

        @pl.when(odd == 1)
        def _():
            pl.semaphore_wait(ready, 1)

    def enter_deep():
        @pl.when(odd == 1)
        def _():
            pl.semaphore_wait(barrier, 2 * (deep - 1))
            pl.semaphore_signal(ready, inc=1, device_id={"north": me_n - 1}, device_id_type=MESH)

        @pl.when(odd == 0)
        def _():
            pl.semaphore_wait(ready, 1)

    def north_copy(c, peer):
        p, count, x, size = pieces[c]
        return pltpu.make_async_remote_copy(
            src_ref=x1.at[pl.ds(peer * share_x + x, size), pl.ds(p, count)],
            dst_ref=r.at[me_n, pl.ds(x, size), pl.ds(p, count)],
            send_sem=send_n,
            recv_sem=recv_n.at[c],
            device_id={"north": peer},
            device_id_type=MESH,
        )

    def deep_copy(c, peer):
        p, count, x, size = pieces[c]
        return pltpu.make_async_remote_copy(
            src_ref=s.at[peer, pl.ds(x, size), pl.ds(p, count)],
            dst_ref=t.at[me_d, pl.ds(x, size), pl.ds(p, count)],
            send_sem=send_d,
            recv_sem=recv_d.at[owner[c]],
            device_id={"deep": peer},
            device_id_type=MESH,
        )

    def north_arrived(c):
        p, count, x, size = pieces[c]
        part = r.at[pl.ds(0, north - 1), pl.ds(x, size), pl.ds(p, count)]
        pltpu.make_async_copy(part, part, recv_n.at[c]).wait()

    def deep_arrived(c):
        part = t.at[pl.ds(0, deep - 1), pl.ds(starts[c], chunks[c])]
        pltpu.make_async_copy(part, part, recv_d.at[c]).wait()

    def all_sent():
        part = r.at[pl.ds(0, north - 1)]
        pltpu.make_async_copy(part, part, send_n).wait()
        part = t.at[pl.ds(0, deep - 1)]
        pltpu.make_async_copy(part, part, send_d).wait()

    loads[0].wait()
    for p in range(packs):
        loads[1 + p].wait()
        for y in range(0, share_y, 2):
            rows = [a[p * pack + f, y + i] for i in range(2) for f in range(pack)]
            high, low = split(jnp.concatenate(rows, axis=0))
            lines = lax.dot_general(
                tx[...],
                jnp.concatenate([high, low], axis=1),
                dimension_numbers=(((1,), (1,)), ((), ())),
                preferred_element_type=F32,
            )
            lines = lines[:size_x] + lines[size_x:]
            x1[:, p, y, :] = lines[:, :LANES]
            x1[:, p, y + 1, :] = lines[:, LANES:]
        if p == 0:
            enter_north()
        for c in range(p * early, (p + 1) * early):
            for peer in peers_n:
                north_copy(c, peer).start()

    for c in range(packs * early, len(pieces)):
        for peer in peers_n:
            north_copy(c, peer).start()

    r[me_n] = x1[pl.ds(me_n * share_x, share_x)]

    for copy in late:
        copy.wait()

    rows_y = lax.broadcasted_iota(jnp.int32, (block_y, size_z), 0)
    base = jnp.broadcast_to(sym_z[...], (block_y, size_z))
    column = jnp.zeros((block_y, size_z), F32)
    for i in range(block_y):
        column = jnp.where(rows_y == i, sym_y[0, me_d * block_y + i], column)
    base = base + column

    for c in range(len(pieces)):
        first, count, start, size = pieces[c]
        north_arrived(c)
        for p in range(first, first + count):
            for x in range(start, start + size, 2):
                width = min(2, start + size - x)
                lines = [
                    jnp.concatenate([r[n, x + i, p] for n in range(north)], axis=0)
                    for i in range(width)
                ]
                high, low = split(jnp.concatenate(lines, axis=1))
                stack = jnp.concatenate([high, high, low], axis=0)
                mixed = jnp.dot(ty[...], stack, preferred_element_type=F32)
                for i in range(width):
                    modes = mixed[:, i * LANES:(i + 1) * LANES]
                    for d in range(deep):
                        s[d, x + i, p] = modes[d * block_y:(d + 1) * block_y]
        if c == 0:
            enter_deep()
        now = across[:-1] + along if c == 0 else along + across[:-1]
        for peer in now:
            deep_copy(c, peer).start()
        held = len(pieces) - min(HOLD, len(pieces))
        for k in [c] if c < held else range(held, len(pieces)) if c == len(pieces) - 1 else []:
            deep_copy(k, across[-1]).start()

    t[me_d] = s[me_d]

    for c in range(len(chunks)):
        weights = []
        for x in range(starts[c], starts[c] + chunks[c]):
            weight = 1.0 / (1.0 + (base + sym_x[0, me_n * share_x + x]))
            weights.append((weight, 1.0 - weight))
        deep_arrived(c)
        height = chunks[c] * block_y
        rows = []
        for p in range(packs):
            lines = [
                t[d, starts[c]:starts[c] + chunks[c], p].reshape(height, LANES) for d in range(deep)
            ]
            for f in range(pack):
                rows.append(
                    jnp.concatenate(
                        [line[:, f * share_z:(f + 1) * share_z] for line in lines], axis=1
                    )
                )
        high, low = split(jnp.concatenate(rows, axis=0))
        main = jnp.dot(jnp.concatenate([high, low], axis=0), tz[0], preferred_element_type=F32)
        rest = jnp.dot(high, tz[1], preferred_element_type=F32)
        spectrum = main[:fields * height] + main[fields * height:] + rest
        for i in range(chunks[c]):
            x = starts[c] + i
            weight, other = weights[i]
            old = [
                spectrum[f * height + i * block_y:f * height + (i + 1) * block_y]
                for f in range(fields)
            ]
            for f in range(fields):
                total = coupling[f, 0] * old[0]
                for g in range(1, fields):
                    total = total + coupling[f, g] * old[g]
                out[f, x] = weight * old[f] + other * total

    all_sent()


def on_device(north, deep, velocity, coupling, symbol_x, symbol_y, symbol_z):
    field = jnp.transpose(velocity, (0, 2, 3, 1))
    fields, share_y, share_z, size_x = field.shape
    size_y, size_z = share_y * north, share_z * deep
    share_x, block_y = size_x // north, size_y // deep
    packs = fields * share_z // LANES
    unit = sum(SIZES)
    chunks = [size * share_x // unit for size in SIZES] if share_x % unit == 0 else [share_x]
    count = len(plan(chunks, packs)[2])
    high, low = basis_table(size_x)
    tx = jnp.asarray(np.block([[high, high], [low, np.zeros_like(low)]]))
    high, low = basis_table(size_y)
    ty = jnp.asarray(np.concatenate([high, low, high], axis=1))
    high, low = basis_table(size_z)
    tz = jnp.asarray(np.stack([high, low]))
    need = 4 * field.size * 7 + 2 * (tx.size + ty.size + tz.size) + 2**21
    vmem = pl.BlockSpec(memory_space=pltpu.VMEM)
    hbm = pl.BlockSpec(memory_space=pltpu.HBM)
    operands = (field, coupling, symbol_x[None, :], symbol_y[None, :], symbol_z[None, :], tx, ty, tz)
    return pl.pallas_call(
        functools.partial(kernel, north, deep, chunks),
        out_shape=jax.ShapeDtypeStruct((fields, share_x, block_y, size_z), F32),
        in_specs=[hbm] * 8,
        out_specs=vmem,
        scratch_shapes=[
            pltpu.VMEM(field.shape, F32),
            pltpu.SMEM(coupling.shape, F32),
            pltpu.SMEM((1, size_x), F32),
            pltpu.SMEM((1, size_y), F32),
            pltpu.VMEM((1, size_z), F32),
            pltpu.VMEM(tx.shape, BF16),
            pltpu.VMEM(ty.shape, BF16),
            pltpu.VMEM(tz.shape, BF16),
            pltpu.VMEM((size_x, packs, share_y, LANES), F32),
            pltpu.VMEM((north, share_x, packs, share_y, LANES), F32),
            pltpu.VMEM((deep, share_x, packs, block_y, LANES), F32),
            pltpu.VMEM((deep, share_x, packs, block_y, LANES), F32),
            pltpu.SemaphoreType.DMA((7 + packs,)),
            pltpu.SemaphoreType.DMA,
            pltpu.SemaphoreType.DMA((count,)),
            pltpu.SemaphoreType.DMA,
            pltpu.SemaphoreType.DMA((len(chunks),)),
            pltpu.SemaphoreType.REGULAR,
        ],
        compiler_params=pltpu.CompilerParams(
            collective_id=0, has_side_effects=True, vmem_limit_bytes=need
        ),
    )(*[pltpu.with_memory_space_constraint(v, pltpu.HBM) for v in operands])


def solution(mesh):
    placed = (P(None, None, "north", "deep"), P(), P(), P(), P())
    return jax.shard_map(
        functools.partial(on_device, mesh.shape["north"], mesh.shape["deep"]),
        mesh=mesh,
        in_specs=placed,
        out_specs=P(None, "north", "deep", None),
        check_vma=False,
    )
```

profile of v0, /device:TPU:9, one launch (start us, length us, event | category | flops | bytes accessed | tf_op | source)
XLA Modules:
  0.0 32.9 jit_solution(17687005232191246249)
XLA Ops:
  0.0 31.9 %shard_map.82 = f32[4,16,16,256]{3,2,1,0:T(8,128)S(1)} custom-call(f32[4,8,64,128]{3,2,1,0:T(8,128)} %bitcast.4, f32[4,4]{1,0:T(4,128)} %coupling_hbm.1, f32[1,128]{1,0:T(1,128)} %bitcast.6, f32[1,64]{1,0:T(1,128)} %bitcast.7, f32[1,256]{1,0:T(1,128)} %bitcast.5, bf16[256,256]{1,0:T(8,128)(2,1)} %constant.6.clone.tx_hbm, ...), custom_call_target="tpu_custom_call" | custom-call | tf_op jit(solution)/shard_map/pallas_call | solution.py:278
  31.9 1.0 %copy.10 = f32[4,16,16,256]{3,2,1,0:T(8,128)} copy(f32[4,16,16,256]{3,2,1,0:T(8,128)S(1)} %shard_map.82) | data formatting | bytes 2097152
where the time goes:
time: 33 us; the launch traced here: 32.9 us
  Pallas kernels  31.9 us (97%)
  local copies, waits for them, and re-layouts  0.97 us (3%)
    pallas_call x1, Pallas kernels, on_device(): pl.pallas_call(functools.partial(kernel, north, deep, chunks), out_shape=...  31.9 us
    unnamed x1, local copies, waits for them, and re-layouts  0.97 us

commit v1 on v0

--- a/solution.py
+++ b/solution.py
@@ -9,9 +9,11 @@
 from jax.sharding import PartitionSpec as P
 
 LANES = 128
-SIZES = (1, 1, 2, 4, 2, 2, 2, 2)
+SIZES = (1, 1, 2, 2, 3, 2, 2, 2, 1)
 EARLY = 2
 HOLD = 4
+PASS = 5
+LENT = 4
 F32 = jnp.float32
 BF16 = jnp.bfloat16
 MESH = pl.DeviceIdType.MESH
@@ -47,7 +49,9 @@
     a_hbm, coupling_hbm, sym_x_hbm, sym_y_hbm, sym_z_hbm, tx_hbm, ty_hbm, tz_hbm,
     out,
     a, coupling, sym_x, sym_y, sym_z, tx, ty, tz, x1, r, s, t,
+    given, r_given, s_given,
     load_sem, send_n, recv_n, send_d, recv_d, ready,
+    send_lent, send_give, recv_give, send_pass, recv_pass, send_given,
 ):
     me_n = lax.axis_index("north")
     me_d = lax.axis_index("deep")
@@ -60,6 +64,11 @@
     size_z = share_z * deep
     starts, early, pieces, owner = plan(chunks, packs)
     half = deep // 2
+    last = len(pieces) - 1
+    split_x = len(chunks) > LENT
+    lent = owner.index(LENT) if split_x else -1
+    first_x, shared = (starts[LENT], chunks[LENT]) if split_x else (0, 1)
+    giver, taker = half, half - 1
     odd = lax.rem(me_n, 2)
 
     loads = [pltpu.make_async_copy(tx_hbm, tx, load_sem.at[0])]
@@ -91,30 +100,36 @@
         def _():
             pl.semaphore_signal(barrier, inc=1, device_id={"north": even}, device_id_type=MESH)
 
+    @pl.when(odd == 0)
+    def _():
+        pl.semaphore_signal(barrier, inc=1, device_id={"north": me_n + 1}, device_id_type=MESH)
+
     for peer in peers_d:
         pl.semaphore_signal(
             barrier, inc=1, device_id={"north": me_n - odd + 1, "deep": peer}, device_id_type=MESH
         )
 
+    def gather_north():
+        pl.semaphore_wait(barrier, north - 1)
+        pl.semaphore_signal(ready, inc=1, device_id={"north": me_n + 1}, device_id_type=MESH)
+
+    def gather_deep():
+        pl.semaphore_wait(barrier, 2 * (deep - 1) + 1)
+        pl.semaphore_signal(ready, inc=1, device_id={"north": me_n - 1}, device_id_type=MESH)
+
+    def be_ready():
+        pl.semaphore_wait(ready, 1)
+
+    gives = lax.convert_element_type(me_d == giver, jnp.int32) if split_x else 0
+
     def enter_north():
-        @pl.when(odd == 0)
-        def _():
-            pl.semaphore_wait(barrier, north - 1)
-            pl.semaphore_signal(ready, inc=1, device_id={"north": me_n + 1}, device_id_type=MESH)
-
-        @pl.when(odd == 1)
-        def _():
-            pl.semaphore_wait(ready, 1)
+        pl.when(odd == 0)(gather_north)
+        pl.when(odd * gives == 1)(gather_deep)
+        pl.when(odd == 1)(be_ready)
 
     def enter_deep():
-        @pl.when(odd == 1)
-        def _():
-            pl.semaphore_wait(barrier, 2 * (deep - 1))
-            pl.semaphore_signal(ready, inc=1, device_id={"north": me_n - 1}, device_id_type=MESH)
-
-        @pl.when(odd == 0)
-        def _():
-            pl.semaphore_wait(ready, 1)
+        pl.when(odd * (1 - gives) == 1)(gather_deep)
+        pl.when(odd == 0)(be_ready)
 
     def north_copy(c, peer):
         p, count, x, size = pieces[c]
@@ -132,26 +147,90 @@
         return pltpu.make_async_remote_copy(
             src_ref=s.at[peer, pl.ds(x, size), pl.ds(p, count)],
             dst_ref=t.at[me_d, pl.ds(x, size), pl.ds(p, count)],
-            send_sem=send_d,
+            send_sem=send_lent if c == lent else send_d,
             recv_sem=recv_d.at[owner[c]],
             device_id={"deep": peer},
             device_id_type=MESH,
         )
 
+    def give(p, k):
+        return pltpu.make_async_remote_copy(
+            src_ref=x1.at[pl.ds(k * share_x + first_x, shared), pl.ds(p, 1)],
+            dst_ref=given.at[k, pl.ds(0, shared), pl.ds(p, 1)],
+            send_sem=send_give,
+            recv_sem=recv_give,
+            device_id={"deep": taker},
+            device_id_type=MESH,
+        )
+
+    def pass_on(peer):
+        return pltpu.make_async_remote_copy(
+            src_ref=given.at[peer],
+            dst_ref=r_given.at[me_n],
+            send_sem=send_pass,
+            recv_sem=recv_pass,
+            device_id={"north": peer},
+            device_id_type=MESH,
+        )
+
+    def hand_over(peer):
+        return pltpu.make_async_remote_copy(
+            src_ref=s_given.at[peer],
+            dst_ref=t.at[giver, pl.ds(first_x, shared)],
+            send_sem=send_given,
+            recv_sem=recv_d.at[LENT],
+            device_id={"deep": peer},
+            device_id_type=MESH,
+        )
+
+    def take(ref, sem):
+        pltpu.make_async_copy(ref, ref, sem).wait()
+
     def north_arrived(c):
         p, count, x, size = pieces[c]
-        part = r.at[pl.ds(0, north - 1), pl.ds(x, size), pl.ds(p, count)]
-        pltpu.make_async_copy(part, part, recv_n.at[c]).wait()
+        take(r.at[pl.ds(0, north - 1), pl.ds(x, size), pl.ds(p, count)], recv_n.at[c])
 
     def deep_arrived(c):
-        part = t.at[pl.ds(0, deep - 1), pl.ds(starts[c], chunks[c])]
-        pltpu.make_async_copy(part, part, recv_d.at[c]).wait()
+        take(t.at[pl.ds(0, deep - 1), pl.ds(starts[c], chunks[c])], recv_d.at[c])
 
     def all_sent():
-        part = r.at[pl.ds(0, north - 1)]
-        pltpu.make_async_copy(part, part, send_n).wait()
-        part = t.at[pl.ds(0, deep - 1)]
-        pltpu.make_async_copy(part, part, send_d).wait()
+        take(r.at[pl.ds(0, north - 1)], send_n)
+        if not split_x:
+            take(t.at[pl.ds(0, deep - 1)], send_d)
+            return
+        take(t.at[pl.ds(0, deep - 1), pl.ds(0, share_x - shared)], send_d)
+
+        @pl.when(me_d == giver)
+        def _():
+            if half > 1:
+                take(t.at[pl.ds(0, half - 1), pl.ds(first_x, shared)], send_lent)
+            take(given, send_give)
+
+        @pl.when(me_d != giver)
+        def _():
+            take(t.at[pl.ds(0, deep - 1), pl.ds(first_x, shared)], send_lent)
+
+        @pl.when(me_d == taker)
+        def _():
+            take(given.at[pl.ds(0, north - 1)], send_pass)
+            if half > 1:
+                take(s_given.at[pl.ds(0, half - 1)], send_given)
+
+    def to_modes(source, target, first, count, start, stop):
+        for p in range(first, first + count):
+            for x in range(start, stop, 2):
+                width = min(2, stop - x)
+                lines = [
+                    jnp.concatenate([source[n, x + i, p] for n in range(north)], axis=0)
+                    for i in range(width)
+                ]
+                high, low = split(jnp.concatenate(lines, axis=1))
+                stack = jnp.concatenate([high, high, low], axis=0)
+                mixed = jnp.dot(ty[...], stack, preferred_element_type=F32)
+                for i in range(width):
+                    modes = mixed[:, i * LANES:(i + 1) * LANES]
+                    for d in range(deep):
+                        target[d, x + i, p] = modes[d * block_y:(d + 1) * block_y]
 
     loads[0].wait()
     for p in range(packs):
@@ -170,13 +249,17 @@
             x1[:, p, y + 1, :] = lines[:, LANES:]
         if p == 0:
             enter_north()
-        for c in range(p * early, (p + 1) * early):
+        sent = range(p * early, (p + 1) * early if p < packs - 1 else len(pieces))
+        for c in sent:
             for peer in peers_n:
                 north_copy(c, peer).start()
-
-    for c in range(packs * early, len(pieces)):
-        for peer in peers_n:
-            north_copy(c, peer).start()
+        if split_x:
+            @pl.when(me_d == giver)
+            def _():
+                if p == 0:
+                    enter_deep()
+                for k in range(north):
+                    give(p, k).start()
 
     r[me_n] = x1[pl.ds(me_n * share_x, share_x)]
 
@@ -192,29 +275,43 @@
 
     for c in range(len(pieces)):
         first, count, start, size = pieces[c]
+        if c == 0:
+            if split_x:
+                pl.when(me_d != giver)(enter_deep)
+            else:
+                enter_deep()
         north_arrived(c)
-        for p in range(first, first + count):
-            for x in range(start, start + size, 2):
-                width = min(2, start + size - x)
-                lines = [
-                    jnp.concatenate([r[n, x + i, p] for n in range(north)], axis=0)
-                    for i in range(width)
-                ]
-                high, low = split(jnp.concatenate(lines, axis=1))
-                stack = jnp.concatenate([high, high, low], axis=0)
-                mixed = jnp.dot(ty[...], stack, preferred_element_type=F32)
-                for i in range(width):
-                    modes = mixed[:, i * LANES:(i + 1) * LANES]
-                    for d in range(deep):
-                        s[d, x + i, p] = modes[d * block_y:(d + 1) * block_y]
-        if c == 0:
-            enter_deep()
-        now = across[:-1] + along if c == 0 else along + across[:-1]
-        for peer in now:
-            deep_copy(c, peer).start()
+        to_modes(r, s, first, count, start, start + size)
+        crossing = [(c, peer, True) for peer in across[:-1]]
+        beside = [(c, peer, False) for peer in along]
+        now = crossing + beside if c == 0 else beside + crossing
         held = len(pieces) - min(HOLD, len(pieces))
-        for k in [c] if c < held else range(held, len(pieces)) if c == len(pieces) - 1 else []:
-            deep_copy(k, across[-1]).start()
+        then = [c] if c < held else range(held, len(pieces)) if c == last else []
+        for k, peer, crosses in now + [(k, across[-1], True) for k in then]:
+            copy = deep_copy(k, peer)
+            if k == lent and crosses:
+                pl.when(me_d != giver)(copy.start)
+            else:
+                copy.start()
+
+        if split_x and c == min(PASS, last):
+            @pl.when(me_d == taker)
+            def _():
+                take(given, recv_give)
+                for peer in peers_n:
+                    pass_on(peer).start()
+                r_given[me_n] = given[me_n]
+
+    if split_x:
+        @pl.when(me_d == taker)
+        def _():
+            take(r_given.at[pl.ds(0, north - 1)], recv_pass)
+            to_modes(r_given, s_given, 0, packs, 0, shared)
+            for peer in along:
+                hand_over(peer).start()
+            pltpu.make_async_copy(
+                s_given.at[me_d], t.at[giver, pl.ds(first_x, shared)], recv_d.at[LENT]
+            ).start()
 
     t[me_d] = s[me_d]
 
@@ -265,13 +362,14 @@
     unit = sum(SIZES)
     chunks = [size * share_x // unit for size in SIZES] if share_x % unit == 0 else [share_x]
     count = len(plan(chunks, packs)[2])
+    lent = chunks[LENT] if len(chunks) > LENT else 1
     high, low = basis_table(size_x)
     tx = jnp.asarray(np.block([[high, high], [low, np.zeros_like(low)]]))
     high, low = basis_table(size_y)
     ty = jnp.asarray(np.concatenate([high, low, high], axis=1))
     high, low = basis_table(size_z)
     tz = jnp.asarray(np.stack([high, low]))
-    need = 4 * field.size * 7 + 2 * (tx.size + ty.size + tz.size) + 2**21
+    need = 4 * field.size * 8 + 2 * (tx.size + ty.size + tz.size) + 2**21
     vmem = pl.BlockSpec(memory_space=pltpu.VMEM)
     hbm = pl.BlockSpec(memory_space=pltpu.HBM)
     operands = (field, coupling, symbol_x[None, :], symbol_y[None, :], symbol_z[None, :], tx, ty, tz)
@@ -293,12 +391,21 @@
             pltpu.VMEM((north, share_x, packs, share_y, LANES), F32),
             pltpu.VMEM((deep, share_x, packs, block_y, LANES), F32),
             pltpu.VMEM((deep, share_x, packs, block_y, LANES), F32),
+            pltpu.VMEM((north, lent, packs, share_y, LANES), F32),
+            pltpu.VMEM((north, lent, packs, share_y, LANES), F32),
+            pltpu.VMEM((deep, lent, packs, block_y, LANES), F32),
             pltpu.SemaphoreType.DMA((7 + packs,)),
             pltpu.SemaphoreType.DMA,
             pltpu.SemaphoreType.DMA((count,)),
             pltpu.SemaphoreType.DMA,
             pltpu.SemaphoreType.DMA((len(chunks),)),
             pltpu.SemaphoreType.REGULAR,
+            pltpu.SemaphoreType.DMA,
+            pltpu.SemaphoreType.DMA,
+            pltpu.SemaphoreType.DMA,
+            pltpu.SemaphoreType.DMA,
+            pltpu.SemaphoreType.DMA,
+            pltpu.SemaphoreType.DMA,
         ],
         compiler_params=pltpu.CompilerParams(
             collective_id=0, has_side_effects=True, vmem_limit_bytes=need

time: 33 us -> 31.9 us (0.967)
  Pallas kernels: 31.9 us -> 30.7 us
    pallas_call x1, Pallas kernels: 31.9 us -> 30.7 us  [on_device(): pl.pallas_call(functools.partial(kernel, north, deep, chunks), out_shape=...]
where the time goes in v1:
time: 31.9 us; the launch traced here: 31.7 us
  Pallas kernels  30.7 us (96%)
  local copies, waits for them, and re-layouts  0.97 us (3%)
    pallas_call x1, Pallas kernels, on_device(): pl.pallas_call(functools.partial(kernel, north, deep, chunks), out_shape=...  30.7 us
    unnamed x1, local copies, waits for them, and re-layouts  0.97 us

profile of v1, /device:TPU:9, one launch (start us, length us, event | category | flops | bytes accessed | tf_op | source)
XLA Modules:
  0.0 31.7 jit_solution(8230452371154073049)
XLA Ops:
  0.0 30.7 %shard_map.82 = f32[4,16,16,256]{3,2,1,0:T(8,128)S(1)} custom-call(f32[4,8,64,128]{3,2,1,0:T(8,128)} %bitcast.4, f32[4,4]{1,0:T(4,128)} %coupling_hbm.1, f32[1,128]{1,0:T(1,128)} %bitcast.6, f32[1,64]{1,0:T(1,128)} %bitcast.7, f32[1,256]{1,0:T(1,128)} %bitcast.5, bf16[256,256]{1,0:T(8,128)(2,1)} %constant.6.clone.tx_hbm, ...), custom_call_target="tpu_custom_call" | custom-call | tf_op jit(solution)/shard_map/pallas_call | solution.py:376
  30.7 1.0 %copy.10 = f32[4,16,16,256]{3,2,1,0:T(8,128)} copy(f32[4,16,16,256]{3,2,1,0:T(8,128)S(1)} %shard_map.82) | data formatting | bytes 2097152

commit v2 on v1

--- a/solution.py
+++ b/solution.py
@@ -11,8 +11,8 @@
 LANES = 128
 SIZES = (1, 1, 2, 2, 3, 2, 2, 2, 1)
 EARLY = 2
-HOLD = 4
-PASS = 5
+HOLD = 5
+PASS = 4
 LENT = 4
 F32 = jnp.float32
 BF16 = jnp.bfloat16
@@ -68,7 +68,8 @@
     split_x = len(chunks) > LENT
     lent = owner.index(LENT) if split_x else -1
     first_x, shared = (starts[LENT], chunks[LENT]) if split_x else (0, 1)
-    giver, taker = half, half - 1
+    upper, lower = me_d == half, me_d == half - 1
+    inner, partner = upper | lower, deep - 1 - me_d
     odd = lax.rem(me_n, 2)
 
     loads = [pltpu.make_async_copy(tx_hbm, tx, load_sem.at[0])]
@@ -88,7 +89,7 @@
 
     peers_n = [lax.rem(me_n + k, north) for k in range(1, north)]
     side = me_d // half
-    across = [(1 - side) * half + j for j in range(half)]
+    across = [(1 - side) * (deep - 1 - j) + side * j for j in range(half)]
     along = [side * half + lax.rem(me_d + j, half) for j in range(1, half)]
     peers_d = across + along
 
@@ -120,15 +121,12 @@
     def be_ready():
         pl.semaphore_wait(ready, 1)
 
-    gives = lax.convert_element_type(me_d == giver, jnp.int32) if split_x else 0
-
     def enter_north():
         pl.when(odd == 0)(gather_north)
-        pl.when(odd * gives == 1)(gather_deep)
         pl.when(odd == 1)(be_ready)
 
     def enter_deep():
-        pl.when(odd * (1 - gives) == 1)(gather_deep)
+        pl.when(odd == 1)(gather_deep)
         pl.when(odd == 0)(be_ready)
 
     def north_copy(c, peer):
@@ -153,15 +151,21 @@
             device_id_type=MESH,
         )
 
-    def give(p, k):
-        return pltpu.make_async_remote_copy(
-            src_ref=x1.at[pl.ds(k * share_x + first_x, shared), pl.ds(p, 1)],
-            dst_ref=given.at[k, pl.ds(0, shared), pl.ds(p, 1)],
-            send_sem=send_give,
-            recv_sem=recv_give,
-            device_id={"deep": taker},
-            device_id_type=MESH,
-        )
+    def give(given_packs):
+        for p in given_packs:
+            for k in range(north):
+                pltpu.make_async_remote_copy(
+                    src_ref=x1.at[pl.ds(k * share_x + first_x, shared), pl.ds(p, 1)],
+                    dst_ref=given.at[k, pl.ds(0, shared), pl.ds(p, 1)],
+                    send_sem=send_give,
+                    recv_sem=recv_give,
+                    device_id={"deep": partner},
+                    device_id_type=MESH,
+                ).start()
+
+    def enter_and_give(given_packs):
+        enter_deep()
+        give(given_packs)
 
     def pass_on(peer):
         return pltpu.make_async_remote_copy(
@@ -176,12 +180,18 @@
     def hand_over(peer):
         return pltpu.make_async_remote_copy(
             src_ref=s_given.at[peer],
-            dst_ref=t.at[giver, pl.ds(first_x, shared)],
+            dst_ref=t.at[partner, pl.ds(first_x, shared)],
             send_sem=send_given,
             recv_sem=recv_d.at[LENT],
             device_id={"deep": peer},
             device_id_type=MESH,
         )
+
+    def take_and_pass():
+        take(given, recv_give)
+        for peer in peers_n:
+            pass_on(peer).start()
+        r_given[me_n] = given[me_n]
 
     def take(ref, sem):
         pltpu.make_async_copy(ref, ref, sem).wait()
@@ -200,21 +210,17 @@
             return
         take(t.at[pl.ds(0, deep - 1), pl.ds(0, share_x - shared)], send_d)
 
-        @pl.when(me_d == giver)
+        @pl.when(inner)
         def _():
+            take(given, send_give)
+            take(given.at[pl.ds(0, north - 1)], send_pass)
             if half > 1:
                 take(t.at[pl.ds(0, half - 1), pl.ds(first_x, shared)], send_lent)
-            take(given, send_give)
-
-        @pl.when(me_d != giver)
+                take(s_given.at[pl.ds(0, half - 1)], send_given)
+
+        @pl.when(jnp.logical_not(inner))
         def _():
             take(t.at[pl.ds(0, deep - 1), pl.ds(first_x, shared)], send_lent)
-
-        @pl.when(me_d == taker)
-        def _():
-            take(given.at[pl.ds(0, north - 1)], send_pass)
-            if half > 1:
-                take(s_given.at[pl.ds(0, half - 1)], send_given)
 
     def to_modes(source, target, first, count, start, stop):
         for p in range(first, first + count):
@@ -248,18 +254,20 @@
             x1[:, p, y, :] = lines[:, :LANES]
             x1[:, p, y + 1, :] = lines[:, LANES:]
         if p == 0:
+            waits = me_n < north - 2
+            if split_x:
+                pl.when(upper & waits)(functools.partial(enter_and_give, [p]))
             enter_north()
         sent = range(p * early, (p + 1) * early if p < packs - 1 else len(pieces))
         for c in sent:
             for peer in peers_n:
                 north_copy(c, peer).start()
-        if split_x:
-            @pl.when(me_d == giver)
-            def _():
-                if p == 0:
-                    enter_deep()
-                for k in range(north):
-                    give(p, k).start()
+        if split_x and p == 0:
+            pl.when(upper & jnp.logical_not(waits))(functools.partial(enter_and_give, [p]))
+        elif split_x:
+            pl.when(upper)(functools.partial(give, [p]))
+    if split_x:
+        pl.when(lower)(functools.partial(enter_and_give, range(packs)))
 
     r[me_n] = x1[pl.ds(me_n * share_x, share_x)]
 
@@ -277,7 +285,7 @@
         first, count, start, size = pieces[c]
         if c == 0:
             if split_x:
-                pl.when(me_d != giver)(enter_deep)
+                pl.when(jnp.logical_not(inner))(enter_deep)
             else:
                 enter_deep()
         north_arrived(c)
@@ -290,27 +298,25 @@
         for k, peer, crosses in now + [(k, across[-1], True) for k in then]:
             copy = deep_copy(k, peer)
             if k == lent and crosses:
-                pl.when(me_d != giver)(copy.start)
+                pl.when(jnp.logical_not(inner))(copy.start)
             else:
                 copy.start()
 
         if split_x and c == min(PASS, last):
-            @pl.when(me_d == taker)
-            def _():
-                take(given, recv_give)
-                for peer in peers_n:
-                    pass_on(peer).start()
-                r_given[me_n] = given[me_n]
+            pl.when(lower)(take_and_pass)
 
     if split_x:
-        @pl.when(me_d == taker)
+        pl.when(upper)(take_and_pass)
+
+    if split_x:
+        @pl.when(inner)
         def _():
             take(r_given.at[pl.ds(0, north - 1)], recv_pass)
             to_modes(r_given, s_given, 0, packs, 0, shared)
             for peer in along:
                 hand_over(peer).start()
             pltpu.make_async_copy(
-                s_given.at[me_d], t.at[giver, pl.ds(first_x, shared)], recv_d.at[LENT]
+                s_given.at[me_d], t.at[partner, pl.ds(first_x, shared)], recv_d.at[LENT]
             ).start()
 
     t[me_d] = s[me_d]

time: 31.9 us -> 31.7 us (level)
  the two profiles are of different devices: /device:TPU:9 before, /device:TPU:16 now
where the time goes in v2:
time: 31.7 us; the launch traced here: 31.6 us
  Pallas kernels  30.6 us (97%)
  local copies, waits for them, and re-layouts  0.97 us (3%)
    pallas_call x1, Pallas kernels, on_device(): pl.pallas_call(functools.partial(kernel, north, deep, chunks), out_shape=...  30.6 us
    unnamed x1, local copies, waits for them, and re-layouts  0.97 us

profile of v2, /device:TPU:16, one launch (start us, length us, event | category | flops | bytes accessed | tf_op | source)
XLA Modules:
  0.0 31.6 jit_solution(16710300162004723934)
XLA Ops:
  0.0 30.6 %shard_map.82 = f32[4,16,16,256]{3,2,1,0:T(8,128)S(1)} custom-call(f32[4,8,64,128]{3,2,1,0:T(8,128)} %bitcast.4, f32[4,4]{1,0:T(4,128)} %coupling_hbm.1, f32[1,128]{1,0:T(1,128)} %bitcast.6, f32[1,64]{1,0:T(1,128)} %bitcast.7, f32[1,256]{1,0:T(1,128)} %bitcast.5, bf16[256,256]{1,0:T(8,128)(2,1)} %constant.6.clone.tx_hbm, ...), custom_call_target="tpu_custom_call" | custom-call | tf_op jit(solution)/shard_map/pallas_call | solution.py:382
  30.6 1.0 %copy.10 = f32[4,16,16,256]{3,2,1,0:T(8,128)} copy(f32[4,16,16,256]{3,2,1,0:T(8,128)S(1)} %shard_map.82) | data formatting | bytes 2097152

commit v3 on v2

--- a/solution.py
+++ b/solution.py
@@ -9,10 +9,10 @@
 from jax.sharding import PartitionSpec as P
 
 LANES = 128
-SIZES = (1, 1, 2, 2, 3, 2, 2, 2, 1)
+SIZES = (1, 1, 2, 2, 2, 1, 2, 2, 2, 1)
 EARLY = 2
 HOLD = 5
-PASS = 4
+PASS = 6
 LENT = 4
 F32 = jnp.float32
 BF16 = jnp.bfloat16
@@ -65,11 +65,13 @@
     starts, early, pieces, owner = plan(chunks, packs)
     half = deep // 2
     last = len(pieces) - 1
-    split_x = len(chunks) > LENT
-    lent = owner.index(LENT) if split_x else -1
-    first_x, shared = (starts[LENT], chunks[LENT]) if split_x else (0, 1)
+    split_x = len(chunks) > LENT + 1
+    first_x = starts[LENT] if split_x else 0
+    sizes = chunks[LENT:LENT + 2] if split_x else [1, 1]
+    shared = sum(sizes)
     upper, lower = me_d == half, me_d == half - 1
     inner, partner = upper | lower, deep - 1 - me_d
+    lent = {owner.index(LENT): inner, owner.index(LENT + 1): upper} if split_x else {}
     odd = lax.rem(me_n, 2)
 
     loads = [pltpu.make_async_copy(tx_hbm, tx, load_sem.at[0])]
@@ -89,7 +91,7 @@
 
     peers_n = [lax.rem(me_n + k, north) for k in range(1, north)]
     side = me_d // half
-    across = [(1 - side) * (deep - 1 - j) + side * j for j in range(half)]
+    across = [(1 - side) * half + j for j in range(half)]
     along = [side * half + lax.rem(me_d + j, half) for j in range(1, half)]
     peers_d = across + along
 
@@ -145,53 +147,63 @@
         return pltpu.make_async_remote_copy(
             src_ref=s.at[peer, pl.ds(x, size), pl.ds(p, count)],
             dst_ref=t.at[me_d, pl.ds(x, size), pl.ds(p, count)],
-            send_sem=send_lent if c == lent else send_d,
+            send_sem=send_lent.at[list(lent).index(c)] if c in lent else send_d,
             recv_sem=recv_d.at[owner[c]],
             device_id={"deep": peer},
             device_id_type=MESH,
         )
 
-    def give(given_packs):
+    def give(given_packs, size):
         for p in given_packs:
             for k in range(north):
                 pltpu.make_async_remote_copy(
-                    src_ref=x1.at[pl.ds(k * share_x + first_x, shared), pl.ds(p, 1)],
-                    dst_ref=given.at[k, pl.ds(0, shared), pl.ds(p, 1)],
+                    src_ref=x1.at[pl.ds(k * share_x + first_x, size), pl.ds(p, 1)],
+                    dst_ref=given.at[k, pl.ds(0, size), pl.ds(p, 1)],
                     send_sem=send_give,
                     recv_sem=recv_give,
                     device_id={"deep": partner},
                     device_id_type=MESH,
                 ).start()
 
-    def enter_and_give(given_packs):
+    def enter_and_give(given_packs, size):
         enter_deep()
-        give(given_packs)
-
-    def pass_on(peer):
+        give(given_packs, size)
+
+    def pass_on(peer, size):
         return pltpu.make_async_remote_copy(
-            src_ref=given.at[peer],
-            dst_ref=r_given.at[me_n],
+            src_ref=given.at[peer, pl.ds(0, size)],
+            dst_ref=r_given.at[me_n, pl.ds(0, size)],
             send_sem=send_pass,
             recv_sem=recv_pass,
             device_id={"north": peer},
             device_id_type=MESH,
         )
 
-    def hand_over(peer):
-        return pltpu.make_async_remote_copy(
-            src_ref=s_given.at[peer],
-            dst_ref=t.at[partner, pl.ds(first_x, shared)],
-            send_sem=send_given,
-            recv_sem=recv_d.at[LENT],
-            device_id={"deep": peer},
-            device_id_type=MESH,
-        )
-
-    def take_and_pass():
-        take(given, recv_give)
+    def take_and_pass(size):
+        take(given.at[pl.ds(0, north), pl.ds(0, size)], recv_give)
         for peer in peers_n:
-            pass_on(peer).start()
-        r_given[me_n] = given[me_n]
+            pass_on(peer, size).start()
+        r_given[me_n, 0:size] = given[me_n, 0:size]
+
+    def transform_passed(size):
+        take(r_given.at[pl.ds(0, north - 1), pl.ds(0, size)], recv_pass)
+        to_modes(r_given, s_given, 0, packs, 0, size)
+        x = 0
+        for i in range(2 if size == shared else 1):
+            part = pl.ds(x, sizes[i])
+            place = t.at[partner, pl.ds(first_x + x, sizes[i])]
+            arrival = recv_d.at[LENT + i]
+            for peer in along:
+                pltpu.make_async_remote_copy(
+                    src_ref=s_given.at[peer, part],
+                    dst_ref=place,
+                    send_sem=send_given,
+                    recv_sem=arrival,
+                    device_id={"deep": peer},
+                    device_id_type=MESH,
+                ).start()
+            pltpu.make_async_copy(s_given.at[me_d, part], place, arrival).start()
+            x += sizes[i]
 
     def take(ref, sem):
         pltpu.make_async_copy(ref, ref, sem).wait()
@@ -210,17 +222,27 @@
             return
         take(t.at[pl.ds(0, deep - 1), pl.ds(0, share_x - shared)], send_d)
 
-        @pl.when(inner)
+        def settle(gave, took, others):
+            take(given.at[pl.ds(0, north), pl.ds(0, gave)], send_give)
+            take(given.at[pl.ds(0, north - 1), pl.ds(0, took)], send_pass)
+            if half > 1:
+                take(s_given.at[pl.ds(0, half - 1), pl.ds(0, took)], send_given)
+            for i, count in enumerate(others):
+                if count:
+                    take(t.at[pl.ds(0, count), pl.ds(0, sizes[i])], send_lent.at[i])
+
+        @pl.when(upper)
         def _():
-            take(given, send_give)
-            take(given.at[pl.ds(0, north - 1)], send_pass)
-            if half > 1:
-                take(t.at[pl.ds(0, half - 1), pl.ds(first_x, shared)], send_lent)
-                take(s_given.at[pl.ds(0, half - 1)], send_given)
+            settle(shared, sizes[0], [half - 1, half - 1])
+
+        @pl.when(lower)
+        def _():
+            settle(sizes[0], shared, [half - 1, deep - 1])
 
         @pl.when(jnp.logical_not(inner))
         def _():
-            take(t.at[pl.ds(0, deep - 1), pl.ds(first_x, shared)], send_lent)
+            for i in range(2):
+                take(t.at[pl.ds(0, deep - 1), pl.ds(0, sizes[i])], send_lent.at[i])
 
     def to_modes(source, target, first, count, start, stop):
         for p in range(first, first + count):
@@ -256,18 +278,18 @@
         if p == 0:
             waits = me_n < north - 2
             if split_x:
-                pl.when(upper & waits)(functools.partial(enter_and_give, [p]))
+                pl.when(upper & waits)(functools.partial(enter_and_give, [p], shared))
             enter_north()
         sent = range(p * early, (p + 1) * early if p < packs - 1 else len(pieces))
         for c in sent:
             for peer in peers_n:
                 north_copy(c, peer).start()
         if split_x and p == 0:
-            pl.when(upper & jnp.logical_not(waits))(functools.partial(enter_and_give, [p]))
+            pl.when(upper & jnp.logical_not(waits))(functools.partial(enter_and_give, [p], shared))
         elif split_x:
-            pl.when(upper)(functools.partial(give, [p]))
+            pl.when(upper)(functools.partial(give, [p], shared))
     if split_x:
-        pl.when(lower)(functools.partial(enter_and_give, range(packs)))
+        pl.when(lower)(functools.partial(enter_and_give, range(packs), sizes[0]))
 
     r[me_n] = x1[pl.ds(me_n * share_x, share_x)]
 
@@ -297,27 +319,18 @@
         then = [c] if c < held else range(held, len(pieces)) if c == last else []
         for k, peer, crosses in now + [(k, across[-1], True) for k in then]:
             copy = deep_copy(k, peer)
-            if k == lent and crosses:
-                pl.when(jnp.logical_not(inner))(copy.start)
+            if k in lent and crosses:
+                pl.when(jnp.logical_not(lent[k]))(copy.start)
             else:
                 copy.start()
 
         if split_x and c == min(PASS, last):
-            pl.when(lower)(take_and_pass)
+            pl.when(lower)(functools.partial(take_and_pass, shared))
 
     if split_x:
-        pl.when(upper)(take_and_pass)
-
-    if split_x:
-        @pl.when(inner)
-        def _():
-            take(r_given.at[pl.ds(0, north - 1)], recv_pass)
-            to_modes(r_given, s_given, 0, packs, 0, shared)
-            for peer in along:
-                hand_over(peer).start()
-            pltpu.make_async_copy(
-                s_given.at[me_d], t.at[partner, pl.ds(first_x, shared)], recv_d.at[LENT]
-            ).start()
+        pl.when(upper)(functools.partial(take_and_pass, sizes[0]))
+        pl.when(lower)(functools.partial(transform_passed, shared))
+        pl.when(upper)(functools.partial(transform_passed, sizes[0]))
 
     t[me_d] = s[me_d]
 
@@ -368,7 +381,7 @@
     unit = sum(SIZES)
     chunks = [size * share_x // unit for size in SIZES] if share_x % unit == 0 else [share_x]
     count = len(plan(chunks, packs)[2])
-    lent = chunks[LENT] if len(chunks) > LENT else 1
+    lent = sum(chunks[LENT:LENT + 2]) if len(chunks) > LENT + 1 else 1
     high, low = basis_table(size_x)
     tx = jnp.asarray(np.block([[high, high], [low, np.zeros_like(low)]]))
     high, low = basis_table(size_y)
@@ -406,7 +419,7 @@
             pltpu.SemaphoreType.DMA,
             pltpu.SemaphoreType.DMA((len(chunks),)),
             pltpu.SemaphoreType.REGULAR,
-            pltpu.SemaphoreType.DMA,
+            pltpu.SemaphoreType.DMA((2,)),
             pltpu.SemaphoreType.DMA,
             pltpu.SemaphoreType.DMA,
             pltpu.SemaphoreType.DMA,

time: 31.7 us -> 31.1 us (0.981)
  the two profiles are of different devices: /device:TPU:16 before, /device:TPU:9 now
where the time goes in v3:
time: 31.1 us; the launch traced here: 30.9 us
  Pallas kernels  29.9 us (96%)
  local copies, waits for them, and re-layouts  0.97 us (3%)
    pallas_call x1, Pallas kernels, on_device(): pl.pallas_call(functools.partial(kernel, north, deep, chunks), out_shape=...  29.9 us
    unnamed x1, local copies, waits for them, and re-layouts  0.97 us

profile of v3, /device:TPU:9, one launch (start us, length us, event | category | flops | bytes accessed | tf_op | source)
XLA Modules:
  0.0 30.9 jit_solution(8200739700895951292)
XLA Ops:
  0.0 29.9 %shard_map.82 = f32[4,16,16,256]{3,2,1,0:T(8,128)S(1)} custom-call(f32[4,8,64,128]{3,2,1,0:T(8,128)} %bitcast.4, f32[4,4]{1,0:T(4,128)} %coupling_hbm.1, f32[1,128]{1,0:T(1,128)} %bitcast.6, f32[1,64]{1,0:T(1,128)} %bitcast.7, f32[1,256]{1,0:T(1,128)} %bitcast.5, bf16[256,256]{1,0:T(8,128)(2,1)} %constant.6.clone.tx_hbm, ...), custom_call_target="tpu_custom_call" | custom-call | tf_op jit(solution)/shard_map/pallas_call | solution.py:395
  29.9 1.0 %copy.10 = f32[4,16,16,256]{3,2,1,0:T(8,128)} copy(f32[4,16,16,256]{3,2,1,0:T(8,128)S(1)} %shard_map.82) | data formatting | bytes 2097152

commit v4 on v3

--- a/solution.py
+++ b/solution.py
@@ -9,11 +9,10 @@
 from jax.sharding import PartitionSpec as P
 
 LANES = 128
-SIZES = (1, 1, 2, 2, 2, 1, 2, 2, 2, 1)
-EARLY = 2
+SIZES = (2, 2, 2, 2, 1, 2, 2, 1, 2)
 HOLD = 5
-PASS = 6
-LENT = 4
+PASS = 5
+LENT = 3
 F32 = jnp.float32
 BF16 = jnp.bfloat16
 MESH = pl.DeviceIdType.MESH
@@ -37,18 +36,67 @@
 
 def plan(chunks, packs):
     starts = [sum(chunks[:c]) for c in range(len(chunks))]
-    early = min(EARLY, len(chunks))
-    pieces = [(p, 1, starts[c], chunks[c]) for p in range(packs) for c in range(early)]
-    pieces += [(0, packs, starts[c], chunks[c]) for c in range(early, len(chunks))]
-    owner = list(range(early)) * packs + list(range(early, len(chunks)))
+    step = 1 if chunks[0] <= 4 else chunks[0]
+    pieces = [(0, 1, x, step) for x in range(0, chunks[0], step)]
+    pieces += [(p, 1, 0, chunks[0]) for p in range(1, packs)]
+    early = len(pieces)
+    pieces += [(0, packs, starts[c], chunks[c]) for c in range(1, len(chunks))]
+    owner = [0] * early + list(range(1, len(chunks)))
     return starts, early, pieces, owner
+
+
+def to_spectrum(t, tz, start, count, fields):
+    deep, _, packs, block_y, _ = t.shape
+    pack = fields // packs
+    share_z = LANES // pack
+    height = count * block_y
+    rows = []
+    for p in range(packs):
+        lines = [t[d, start:start + count, p].reshape(height, LANES) for d in range(deep)]
+        for f in range(pack):
+            rows.append(
+                jnp.concatenate([line[:, f * share_z:(f + 1) * share_z] for line in lines], axis=1)
+            )
+    high, low = split(jnp.concatenate(rows, axis=0))
+    main = jnp.dot(jnp.concatenate([high, low], axis=0), tz[0], preferred_element_type=F32)
+    rest = jnp.dot(high, tz[1], preferred_element_type=F32)
+    whole = main[:fields * height] + main[fields * height:] + rest
+    return [whole[f * height:(f + 1) * height] for f in range(fields)]
+
+
+def finish(values, last_lines, last_weight, mixing, tz, out, tail, sem):
+    fields, share_x, block_y, _ = values.shape
+    count = last_weight.shape[0]
+    first = share_x - count
+    bulk = pltpu.make_async_copy(
+        values.at[pl.ds(0, fields), pl.ds(0, first)], out.at[pl.ds(0, fields), pl.ds(0, first)],
+        sem.at[0],
+    )
+    bulk.start()
+    spectrum = to_spectrum(last_lines, tz, 0, count, fields)
+    for i in range(count):
+        for y in range(0, block_y, 8):
+            weight = last_weight[i, y:y + 8]
+            other = 1.0 - weight
+            old = [value[i * block_y + y:i * block_y + y + 8] for value in spectrum]
+            for f in range(fields):
+                total = mixing[f, 0] * old[0]
+                for g in range(1, fields):
+                    total = total + mixing[f, g] * old[g]
+                tail[f, i, y:y + 8] = weight * old[f] + other * total
+    rest = pltpu.make_async_copy(
+        tail, out.at[pl.ds(0, fields), pl.ds(first, count)], sem.at[1]
+    )
+    rest.start()
+    bulk.wait()
+    rest.wait()
 
 
 def kernel(
     north, deep, chunks,
     a_hbm, coupling_hbm, sym_x_hbm, sym_y_hbm, sym_z_hbm, tx_hbm, ty_hbm, tz_hbm,
-    out,
-    a, coupling, sym_x, sym_y, sym_z, tx, ty, tz, x1, r, s, t,
+    out, last_lines, last_weight, mixing, tz,
+    a, coupling, sym_x, sym_y, sym_z, tx, ty, x1, r, s, t,
     given, r_given, s_given,
     load_sem, send_n, recv_n, send_d, recv_d, ready,
     send_lent, send_give, recv_give, send_pass, recv_pass, send_given,
@@ -280,7 +328,8 @@
             if split_x:
                 pl.when(upper & waits)(functools.partial(enter_and_give, [p], shared))
             enter_north()
-        sent = range(p * early, (p + 1) * early if p < packs - 1 else len(pieces))
+        sent = [c for c in range(early) if pieces[c][0] == p]
+        sent += range(early, len(pieces)) if p == packs - 1 else []
         for c in sent:
             for peer in peers_n:
                 north_copy(c, peer).start()
@@ -334,40 +383,30 @@
 
     t[me_d] = s[me_d]
 
+    for f in range(fields):
+        for g in range(fields):
+            mixing[f, g] = jnp.full((8, size_z), coupling[f, g], F32)
+
     for c in range(len(chunks)):
         weights = []
         for x in range(starts[c], starts[c] + chunks[c]):
             weight = 1.0 / (1.0 + (base + sym_x[0, me_n * share_x + x]))
             weights.append((weight, 1.0 - weight))
         deep_arrived(c)
-        height = chunks[c] * block_y
-        rows = []
-        for p in range(packs):
-            lines = [
-                t[d, starts[c]:starts[c] + chunks[c], p].reshape(height, LANES) for d in range(deep)
-            ]
-            for f in range(pack):
-                rows.append(
-                    jnp.concatenate(
-                        [line[:, f * share_z:(f + 1) * share_z] for line in lines], axis=1
-                    )
-                )
-        high, low = split(jnp.concatenate(rows, axis=0))
-        main = jnp.dot(jnp.concatenate([high, low], axis=0), tz[0], preferred_element_type=F32)
-        rest = jnp.dot(high, tz[1], preferred_element_type=F32)
-        spectrum = main[:fields * height] + main[fields * height:] + rest
+        if c == len(chunks) - 1:
+            last_lines[...] = t[:, starts[c]:starts[c] + chunks[c]]
+            for i in range(chunks[c]):
+                last_weight[i] = weights[i][0]
+            continue
+        spectrum = to_spectrum(t, tz, starts[c], chunks[c], fields)
         for i in range(chunks[c]):
-            x = starts[c] + i
             weight, other = weights[i]
-            old = [
-                spectrum[f * height + i * block_y:f * height + (i + 1) * block_y]
-                for f in range(fields)
-            ]
+            old = [value[i * block_y:(i + 1) * block_y] for value in spectrum]
             for f in range(fields):
                 total = coupling[f, 0] * old[0]
                 for g in range(1, fields):
                     total = total + coupling[f, g] * old[g]
-                out[f, x] = weight * old[f] + other * total
+                out[f, starts[c] + i] = weight * old[f] + other * total
 
     all_sent()
 
@@ -392,11 +431,17 @@
     vmem = pl.BlockSpec(memory_space=pltpu.VMEM)
     hbm = pl.BlockSpec(memory_space=pltpu.HBM)
     operands = (field, coupling, symbol_x[None, :], symbol_y[None, :], symbol_z[None, :], tx, ty, tz)
-    return pl.pallas_call(
+    results = pl.pallas_call(
         functools.partial(kernel, north, deep, chunks),
-        out_shape=jax.ShapeDtypeStruct((fields, share_x, block_y, size_z), F32),
+        out_shape=[
+            jax.ShapeDtypeStruct((fields, share_x, block_y, size_z), F32),
+            jax.ShapeDtypeStruct((deep, chunks[-1], packs, block_y, LANES), F32),
+            jax.ShapeDtypeStruct((chunks[-1], block_y, size_z), F32),
+            jax.ShapeDtypeStruct((fields, fields, 8, size_z), F32),
+            jax.ShapeDtypeStruct(tz.shape, BF16),
+        ],
         in_specs=[hbm] * 8,
-        out_specs=vmem,
+        out_specs=[vmem] * 5,
         scratch_shapes=[
             pltpu.VMEM(field.shape, F32),
             pltpu.SMEM(coupling.shape, F32),
@@ -405,7 +450,6 @@
             pltpu.VMEM((1, size_z), F32),
             pltpu.VMEM(tx.shape, BF16),
             pltpu.VMEM(ty.shape, BF16),
-            pltpu.VMEM(tz.shape, BF16),
             pltpu.VMEM((size_x, packs, share_y, LANES), F32),
             pltpu.VMEM((north, share_x, packs, share_y, LANES), F32),
             pltpu.VMEM((deep, share_x, packs, block_y, LANES), F32),
@@ -430,6 +474,17 @@
             collective_id=0, has_side_effects=True, vmem_limit_bytes=need
         ),
     )(*[pltpu.with_memory_space_constraint(v, pltpu.HBM) for v in operands])
+    return pl.pallas_call(
+        finish,
+        out_shape=jax.ShapeDtypeStruct((fields, share_x, block_y, size_z), F32),
+        in_specs=[vmem] * 5,
+        out_specs=hbm,
+        scratch_shapes=[
+            pltpu.VMEM((fields, chunks[-1], block_y, size_z), F32),
+            pltpu.SemaphoreType.DMA((2,)),
+        ],
+        compiler_params=pltpu.CompilerParams(vmem_limit_bytes=need),
+    )(*results)
 
 
 def solution(mesh):

time: 31.1 us -> 30.9 us (level)
  local copies, waits for them, and re-layouts: 0.97 us -> 0 us
  Pallas kernels: 29.9 us -> 30.7 us
    pallas_call x0 -> x1, Pallas kernels: none -> 1 us  [on_device(): pl.pallas_call(finish, out_shape=jax.ShapeDtypeStruct((fields, share_x, b...]
    unnamed x1 -> x0, local copies, waits for them, and re-layouts: 0.97 us -> none
where the time goes in v4:
time: 30.9 us; the launch traced here: 30.7 us
  Pallas kernels  30.7 us (99%)
    pallas_call x1, Pallas kernels, on_device(): pl.pallas_call(functools.partial(kernel, north, deep, chunks), out_shape=...  29.7 us
    pallas_call x1, Pallas kernels, on_device(): pl.pallas_call(finish, out_shape=jax.ShapeDtypeStruct((fields, share_x, b...  1 us

profile of v4, /device:TPU:9, one launch (start us, length us, event | category | flops | bytes accessed | tf_op | source)
XLA Modules:
  0.0 30.7 jit_solution(11741211272818385890)
XLA Ops:
  0.0 29.7 %shard_map.82 = (f32[4,16,16,256]{3,2,1,0:T(8,128)S(1)}, f32[4,2,2,16,128]{4,3,2,1,0:T(8,128)S(1)}, f32[2,16,256]{2,1,0:T(8,128)S(1)}, f32[4,4,8,256]{3,2,1,0:T(8,128)S(1)}, bf16[2,256,256]{2,1,0:T(8,128)(2,1)S(1)}) custom-call(f32[4,8,64,128]{3,2,1,0:T(8,128)} %bitcast.4, f32[4,4]{1,0:T(4,128)} %coupling_hbm.1, f32[1,128]{1,0:T(1,128)} %bitcast.6, ...), custom_call_target="tpu_custom_call" | custom-call | tf_op jit(solution)/shard_map/pallas_call | solution.py:434
  29.7 1.0 %shard_map.83 = f32[4,16,16,256]{3,2,1,0:T(8,128)} custom-call(f32[4,16,16,256]{3,2,1,0:T(8,128)S(1)} %get-tuple-element.10.values, f32[4,2,2,16,128]{4,3,2,1,0:T(8,128)S(1)} %get-tuple-element.11.last_lines, f32[2,16,256]{2,1,0:T(8,128)S(1)} %get-tuple-element.12.last_weight, f32[4,4,8,256]{3,2,1,0:T(8,128)S(1)} %get-tuple-element.13.mixing, ...), custom_call_target="tpu_custom_call" | custom-call | tf_op jit(solution)/shard_map/pallas_call | solution.py:477

commit v5 on v4

--- a/solution.py
+++ b/solution.py
@@ -134,7 +134,7 @@
         pltpu.make_async_copy(source, target, load_sem.at[len(loads) + i])
         for i, (source, target) in enumerate(pairs)
     ]
-    for copy in loads + late:
+    for copy in [loads[1], loads[0]]:
         copy.start()
 
     peers_n = [lax.rem(me_n + k, north) for k in range(1, north)]
@@ -311,6 +311,8 @@
     loads[0].wait()
     for p in range(packs):
         loads[1 + p].wait()
+        for copy in loads[2:] + late if p == 0 else []:
+            copy.start()
         for y in range(0, share_y, 2):
             rows = [a[p * pack + f, y + i] for i in range(2) for f in range(pack)]
             high, low = split(jnp.concatenate(rows, axis=0))

time: 30.9 us -> 30.9 us (level)
  no operation moved by 1% of the time
where the time goes in v5:
time: 30.9 us; the launch traced here: 30.8 us
  Pallas kernels  30.8 us (100%)
    pallas_call x1, Pallas kernels, on_device(): pl.pallas_call(functools.partial(kernel, north, deep, chunks), out_shape=...  29.8 us
    pallas_call x1, Pallas kernels, on_device(): pl.pallas_call(finish, out_shape=jax.ShapeDtypeStruct((fields, share_x, b...  1 us

profile of v5, /device:TPU:9, one launch (start us, length us, event | category | flops | bytes accessed | tf_op | source)
XLA Modules:
  0.0 30.8 jit_solution(6377090085810312437)
XLA Ops:
  0.0 29.8 %shard_map.82 = (f32[4,16,16,256]{3,2,1,0:T(8,128)S(1)}, f32[4,2,2,16,128]{4,3,2,1,0:T(8,128)S(1)}, f32[2,16,256]{2,1,0:T(8,128)S(1)}, f32[4,4,8,256]{3,2,1,0:T(8,128)S(1)}, bf16[2,256,256]{2,1,0:T(8,128)(2,1)S(1)}) custom-call(f32[4,8,64,128]{3,2,1,0:T(8,128)} %bitcast.4, f32[4,4]{1,0:T(4,128)} %coupling_hbm.1, f32[1,128]{1,0:T(1,128)} %bitcast.6, ...), custom_call_target="tpu_custom_call" | custom-call | tf_op jit(solution)/shard_map/pallas_call | solution.py:436
  29.8 1.0 %shard_map.83 = f32[4,16,16,256]{3,2,1,0:T(8,128)} custom-call(f32[4,16,16,256]{3,2,1,0:T(8,128)S(1)} %get-tuple-element.10.values, f32[4,2,2,16,128]{4,3,2,1,0:T(8,128)S(1)} %get-tuple-element.11.last_lines, f32[2,16,256]{2,1,0:T(8,128)S(1)} %get-tuple-element.12.last_weight, f32[4,4,8,256]{3,2,1,0:T(8,128)S(1)} %get-tuple-element.13.mixing, ...), custom_call_target="tpu_custom_call" | custom-call | tf_op jit(solution)/shard_map/pallas_call | solution.py:479
